TPU v7x, 8 devices: a whole 2x2x1 slice. The times are simulated.
8 devices in a mesh: data: 2 (over z, y), tp: 4 (over x, core).
Axes of the slice: x: 2, y: 2, z: 1, core: 2. Of those that a mesh axis runs over, the one named last changes fastest.
Arguments:
- attn_ctx: bfloat16 [4096, 8192], P('data', 'tp'), parts along dimension 0
- w_attn_out: bfloat16 [8192, 8192], P('tp')
- mlp_act: bfloat16 [4096, 32768], P('data', 'tp'), parts along dimension 0
- w_mlp_down: bfloat16 [32768, 8192], P('tp')
Outputs:
- output: bfloat16 [4096, 8192], P('data'), parts along dimension 0
There are 2 independent parts. A program takes and returns all parts, laid end to end along the dimension named above; an argument that names none is the same for every part.
All inputs are finite; a program needn't handle non-finite values.
Results may differ from a plain program's by a relative error of at most 0.0102996.
Values are sent between devices in bfloat16 or wider.
A program may use at most 1 GiB of HBM per device.

v0:
```python
import jax
import jax.numpy as jnp
from jax import lax
from jax.sharding import PartitionSpec as P


def solution(mesh):
    def device_step(ctx_block, w_out_block, act_block, w_down_block):
        part_sum = jnp.dot(ctx_block, w_out_block, preferred_element_type=jnp.float32)
        part_sum = part_sum + jnp.dot(act_block, w_down_block, preferred_element_type=jnp.float32)
        row_sum = lax.psum_scatter(part_sum.astype(jnp.bfloat16), "tp", scatter_dimension=0, tiled=True)
        return lax.all_gather(row_sum, "tp", axis=0, tiled=True)

    return jax.shard_map(
        device_step,
        mesh=mesh,
        in_specs=(P("data", "tp"), P("tp", None), P("data", "tp"), P("tp", None)),
        out_specs=P("data", None),
        check_vma=False,
    )
```

profile of v0, /device:TPU:0, one launch (start us, length us, event | category | flops | bytes accessed | tf_op | source)
XLA Modules:
  0.0 851.7 jit_solution(12219748631065022602)
XLA Ops:
  6.5 0.0 reduce-scatter.4.cloned.1.call-start
  6.5 79.1 %fusion = f32[2048,8192]{1,0:T(8,128)} fusion(bf16[2048,2048]{1,0:T(8,128)(2,1)} %param.4, bf16[2048,8192]{1,0:T(8,128)(2,1)} %param.5), kind=kOutput, calls=%fused_computation.1 | convolution fusion | flops 68719476736 | bytes 109051904 | tf_op jit(solution)/shard_map/dot_general | solution.py:9
  85.6 306.3 %add_convert_fusion = bf16[2048,8192]{1,0:T(8,128)(2,1)} fusion(f32[2048,8192]{1,0:T(8,128)} %fusion, bf16[2048,8192]{1,0:T(8,128)(2,1)} %param.6, bf16[8192,8192]{1,0:T(8,128)(2,1)} %param.7), kind=kOutput, calls=%fused_computation | convolution fusion | flops 274911461376 | bytes 268435456 | tf_op jit(solution)/shard_map/dot_general | solution.py:10
  391.9 0.0 reduce-scatter.4.cloned.1.call-update
  391.9 0.0 all-gather.2.cloned.1.call-start
  392.0 228.9 %reduce-scatter.4.cloned.1.call-done = bf16[512,8192]{1,0:T(8,128)(2,1)} async-done(((bf16[2048,8192]{1,0:T(8,128)(2,1)}), bf16[512,8192]{1,0:T(8,128)(2,1)}) %reduce-scatter.4.cloned.1.call-update) | async-done | bytes 8388624
  620.9 0.0 all-gather.2.cloned.1.call-update
  620.9 200.9 %all-gather.2.cloned.1.call-done = bf16[2048,8192]{1,0:T(8,128)(2,1)} async-done(((bf16[512,8192]{1,0:T(8,128)(2,1)}), bf16[2048,8192]{1,0:T(8,128)(2,1)}) %all-gather.2.cloned.1.call-update) | async-done | bytes 33554448 | tf_op jit(solution)/shard_map/all_gather | solution.py:12
  821.8 23.0 %copy.6 = bf16[2048,8192]{1,0:T(8,128)(2,1)} copy(bf16[2048,8192]{1,0:T(8,128)(2,1)} %all-gather.2.cloned.1.call-done) | data formatting | bytes 67108864
Async XLA Ops:
  6.5 614.4 %reduce-scatter.4.cloned.1.call-start = ((), (), s32[]{:S(2)}) async-start(), calls=%async_computation.2 | async-start | bytes 41943040
  391.9 429.9 %all-gather.2.cloned.1.call-start = ((), (), s32[]{:S(2)}) async-start(), calls=%async_computation.1 | async-start | bytes 41943040 | tf_op jit(solution)/shard_map/all_gather | solution.py:12
Sparse Core Ops, SparseCore 0:
  392.1 228.8 reduce-scatter.3
  622.4 199.3 all-gather.1
where the time goes:
time: 852 us
  waiting for transfers between devices  430 us (50%)
  matrix products  385 us (45%)
  local copies, waits for them, and re-layouts  23 us (3%)
  between operations  13.4 us (2%)
    dot_general x1, matrix products, device_step(): jnp.dot(act_block, w_down_block, preferred_element_type=jnp.float32)  306 us
    unnamed x3, waiting for transfers between devices  229 us
    all_gather x1, waiting for transfers between devices, device_step(): return lax.all_gather(row_sum, 'tp', axis=0, tiled=True)  201 us
    dot_general x1, matrix products, device_step(): jnp.dot(ctx_block, w_out_block, preferred_element_type=jnp.float32)  79.1 us
    unnamed x1, local copies, waits for them, and re-layouts  23 us
  transfers between devices with their start and end apart: 2, of which 2 were waited for; matrix products, arithmetic and copies ran while one was open for 0% of the time, Pallas kernels for 0%

commit v1 on v0

v1 whole, which is shorter than its diff:
```python
import jax
import jax.numpy as jnp
from jax import lax
from jax.experimental import pallas as pl
from jax.experimental.pallas import tpu as pltpu
from jax.sharding import PartitionSpec as P

MESH = pl.DeviceIdType.MESH
COLS = 256
DEPTH = 2048
SLOTS = 4


def _kernel(
    ctx, w_out, act, w_down, y,
    x, w, acc, part, sib_part, chip, far_chip, done,
    x_sem, w_sem, sib_send, sib_recv, far_send, far_recv, y_sem, y_send, y_recv,
    sib_free, far_free,
):
    rows = y.shape[0]
    half = rows // 2
    tiles = y.shape[1] // COLS
    ctx_depth = ctx.shape[1]
    chunks = x.shape[1] // DEPTH
    ctx_chunks = ctx_depth // DEPTH

    me = lax.axis_index("tp")
    core = lax.rem(me, 2)
    sib = {"tp": me + 1 - 2 * core}
    far = {"tp": lax.rem(me + 2, 4)}
    own_row = pl.multiple_of(core * half, half)
    sib_row = pl.multiple_of((1 - core) * half, half)

    def columns(j):
        return pl.ds(pl.multiple_of(j * COLS, COLS), COLS)

    def load_x(part_i, i):
        row = sib_row if part_i == 0 else own_row
        if i < ctx_chunks:
            src = ctx.at[pl.ds(row, half), pl.ds(i * DEPTH, DEPTH)]
        else:
            src = act.at[pl.ds(row, half), pl.ds((i - ctx_chunks) * DEPTH, DEPTH)]
        dst = x.at[pl.ds(part_i * half, half), pl.ds(i * DEPTH, DEPTH)]
        return pltpu.make_async_copy(src, dst, x_sem.at[part_i, i])

    def load_w(j, i):
        s = lax.rem(j, 2)
        if i < ctx_chunks:
            src = w_out.at[pl.ds(i * DEPTH, DEPTH), columns(j)]
        else:
            src = w_down.at[pl.ds((i - ctx_chunks) * DEPTH, DEPTH), columns(j)]
        return pltpu.make_async_copy(src, w.at[s, pl.ds(i * DEPTH, DEPTH), :], w_sem.at[s, i])

    def send_part(j):
        s = lax.rem(j, 2)
        return pltpu.make_async_remote_copy(
            part.at[s], sib_part.at[s], sib_send.at[s], sib_recv.at[s],
            device_id=sib, device_id_type=MESH)

    def send_chip(j):
        s = lax.rem(j, SLOTS)
        return pltpu.make_async_remote_copy(
            chip.at[s], far_chip.at[s], far_send.at[s], far_recv.at[s],
            device_id=far, device_id_type=MESH)

    def store_y(j):
        s = lax.rem(j, 2)
        return pltpu.make_async_copy(done.at[s], y.at[pl.ds(own_row, half), columns(j)], y_sem.at[s])

    def send_y(j):
        s = lax.rem(j, 2)
        return pltpu.make_async_remote_copy(
            done.at[s], y.at[pl.ds(own_row, half), columns(j)],
            y_send.at[s], y_recv.at[lax.rem(j, SLOTS)],
            device_id=sib, device_id_type=MESH)

    def chip_sum(j):
        total = acc[...] + sib_part[lax.rem(j, 2)].astype(jnp.float32)
        chip[lax.rem(j, SLOTS)] = total.astype(jnp.bfloat16)

    def final_sum(j):
        s = lax.rem(j, SLOTS)
        total = chip[s].astype(jnp.float32) + far_chip[s].astype(jnp.float32)
        done[lax.rem(j, 2)] = total.astype(jnp.bfloat16)

    for i in range(chunks):
        load_w(0, i).start()
        load_x(0, i).start()
    for i in range(chunks):
        load_x(1, i).start()
    for i in range(chunks):
        load_w(1, i).start()

    barrier = pltpu.get_barrier_semaphore()
    for peer in (sib, far):
        pl.semaphore_signal(barrier, inc=1, device_id=peer, device_id_type=MESH)
    pl.semaphore_wait(barrier, 2)

    for part_i in range(2):
        for i in range(chunks):
            if part_i == 0:
                load_w(0, i).wait()
            load_x(part_i, i).wait()
            depth = pl.ds(i * DEPTH, DEPTH)
            term = jnp.dot(x[pl.ds(part_i * half, half), depth], w[0, depth, :],
                           preferred_element_type=jnp.float32)
            if i == 0:
                acc[...] = term
            else:
                acc[...] += term
        if part_i == 0:
            part[0] = acc[...].astype(jnp.bfloat16)
            send_part(0).start()

    def wait_chip_inputs(j):
        send_part(j).wait_recv()

        @pl.when(j >= SLOTS)
        def _():
            send_chip(j - SLOTS).wait_send()
            pl.semaphore_wait(far_free, 1)

    def wait_final_inputs(j):
        send_chip(j).wait_recv()

        @pl.when(j >= 2)
        def _():
            store_y(j - 2).wait()
            send_y(j - 2).wait_send()
            send_y(j - 2).wait_recv()

    def finish_chip(j):
        chip_sum(j)
        send_chip(j).start()

    def finish_final(j):
        final_sum(j)
        store_y(j).start()
        send_y(j).start()

    def free_sib(j):
        @pl.when(j + 2 < tiles)
        def _():
            pl.semaphore_signal(sib_free, inc=1, device_id=sib, device_id_type=MESH)

    def free_far(j):
        @pl.when(j + SLOTS < tiles)
        def _():
            pl.semaphore_signal(far_free, inc=1, device_id=far, device_id_type=MESH)

    def tile(j, with_final):
        for i in range(chunks):
            load_w(j, i).wait()
        wait_chip_inputs(j - 1)
        if with_final:
            wait_final_inputs(j - 3)

        @pl.when(j >= 2)
        def _():
            send_part(j - 2).wait_send()
            pl.semaphore_wait(sib_free, 1)

        @pl.when(j + 1 < tiles)
        def _():
            for i in range(chunks):
                load_w(j + 1, i).start()

        s = lax.rem(j, 2)

        def one_half(h, carry):
            @pl.when(h == 0)
            def _():
                finish_chip(j - 1)

            if with_final:
                @pl.when(h == 1)
                def _():
                    finish_final(j - 3)

            row = pl.multiple_of(h * half, half)
            acc[...] = jnp.dot(x[pl.ds(row, half), :], w[s], preferred_element_type=jnp.float32)

            @pl.when(h == 0)
            def _():
                part[s] = acc[...].astype(jnp.bfloat16)
                send_part(j).start()

            return carry

        lax.fori_loop(0, 2, one_half, 0)
        free_sib(j - 1)
        if with_final:
            free_far(j - 3)

    def early(j, carry):
        tile(j, False)
        return carry

    def steady(j, carry):
        tile(j, True)
        return carry

    lax.fori_loop(1, 3, early, 0)
    lax.fori_loop(3, tiles, steady, 0)

    last = tiles - 1
    wait_chip_inputs(last)
    finish_chip(last)
    for j in range(tiles - 3, tiles):
        wait_final_inputs(j)
        finish_final(j)
    for j in range(tiles - 2, tiles):
        store_y(j).wait()
        send_y(j).wait_send()
        send_y(j).wait_recv()
        send_part(j).wait_send()
    for j in range(tiles - SLOTS, tiles):
        send_chip(j).wait_send()


def solution(mesh):
    def device_step(ctx, w_out, act, w_down):
        rows, depth = ctx.shape[0], ctx.shape[1] + act.shape[1]
        half, width = rows // 2, w_out.shape[1]
        piece = (half, COLS)
        sem = pltpu.SemaphoreType.DMA
        return pl.pallas_call(
            _kernel,
            out_shape=jax.ShapeDtypeStruct((rows, width), jnp.bfloat16),
            in_specs=[pl.BlockSpec(memory_space=pl.ANY)] * 4,
            out_specs=pl.BlockSpec(memory_space=pl.ANY),
            scratch_shapes=[
                pltpu.VMEM((rows, depth), jnp.bfloat16),
                pltpu.VMEM((2, depth, COLS), jnp.bfloat16),
                pltpu.VMEM(piece, jnp.float32),
                pltpu.VMEM((2, *piece), jnp.bfloat16),
                pltpu.VMEM((2, *piece), jnp.bfloat16),
                pltpu.VMEM((SLOTS, *piece), jnp.bfloat16),
                pltpu.VMEM((SLOTS, *piece), jnp.bfloat16),
                pltpu.VMEM((2, *piece), jnp.bfloat16),
                sem((2, depth // DEPTH)),
                sem((2, depth // DEPTH)),
                sem((2,)), sem((2,)),
                sem((SLOTS,)), sem((SLOTS,)),
                sem((2,)), sem((2,)), sem((SLOTS,)),
                pltpu.SemaphoreType.REGULAR,
                pltpu.SemaphoreType.REGULAR,
            ],
            compiler_params=pltpu.CompilerParams(
                collective_id=0, has_side_effects=True, vmem_limit_bytes=67043328),
            cost_estimate=pl.CostEstimate(
                flops=2 * rows * depth * width, transcendentals=0,
                bytes_accessed=2 * (rows * depth + depth * width + rows * width)),
        )(ctx, w_out, act, w_down)

    return jax.shard_map(
        device_step,
        mesh=mesh,
        in_specs=(P("data", "tp"), P("tp", None), P("data", "tp"), P("tp", None)),
        out_specs=P("data", None),
        check_vma=False,
    )
```

time: 852 us -> 426 us (0.50)
  waiting for transfers between devices: 430 us -> 0 us
  Pallas kernels: 0 us -> 403 us
  matrix products: 385 us -> 0 us
  between operations: 13.4 us -> 0.01 us
    pallas_call x0 -> x1, Pallas kernels: none -> 403 us  [device_step(): pl.pallas_call(_kernel, out_shape=jax.ShapeDtypeStruct((rows, width), jnp...]
    dot_general x2 -> x0, matrix products: 385 us -> none  [the longest x1 306 us: device_step(): jnp.dot(act_block, w_down_block, preferred_element_type=jnp.float32)]
    unnamed x3 -> x0, waiting for transfers between devices: 229 us -> none
    all_gather x1 -> x0, waiting for transfers between devices: 201 us -> none  [device_step(): return lax.all_gather(row_sum, 'tp', axis=0, tiled=True)]
  transfers between devices with their start and end apart: 2 -> 0, of which waited for: 2 -> 0; matrix products, arithmetic and copies ran while one was open for 0% -> 0% of each run, Pallas kernels for 0% -> 0%
where the time goes in v1:
time: 426 us
  Pallas kernels  403 us (95%)
  local copies, waits for them, and re-layouts  23 us (5%)
    pallas_call x1, Pallas kernels, device_step(): pl.pallas_call(_kernel, out_shape=jax.ShapeDtypeStruct((rows, width), jnp...  403 us
    unnamed x1, local copies, waits for them, and re-layouts  23 us

profile of v1, /device:TPU:0, one launch (start us, length us, event | category | flops | bytes accessed | tf_op | source)
XLA Modules:
  0.0 426.2 jit_solution(13432274783054980044)
XLA Ops:
  0.0 403.2 %shard_map.46 = bf16[2048,8192]{1,0:T(8,128)(2,1)} custom-call(bf16[2048,2048]{1,0:T(8,128)(2,1)} %ctx.1, bf16[2048,8192]{1,0:T(8,128)(2,1)} %w_out.1, bf16[2048,8192]{1,0:T(8,128)(2,1)} %act.1, bf16[8192,8192]{1,0:T(8,128)(2,1)} %w_down.1), custom_call_target="tpu_custom_call" | custom-call | flops 343597383680 | bytes 243269632 | tf_op jit(solution)/shard_map/pallas_call | solution.py:227
  403.2 23.0 %copy.6 = bf16[2048,8192]{1,0:T(8,128)(2,1)} copy(bf16[2048,8192]{1,0:T(8,128)(2,1)} %shard_map.46) | data formatting | bytes 67108864

commit v2 on v0

v2 whole, which is shorter than its diff:
```python
import jax
import jax.numpy as jnp
from jax import lax
from jax.experimental import pallas as pl
from jax.experimental.pallas import tpu as pltpu
from jax.sharding import PartitionSpec as P

MESH = pl.DeviceIdType.MESH
COLS = 256
DEPTH = 2048
LAG = 5
SLOTS = 2 * LAG - 1


def _kernel(
    ctx, w_out, act, w_down, y,
    x, w, sib_acc, acc, part, sib_part, chip, far_chip, done,
    x_sem, w_sem, sib_send, sib_recv, far_send, far_recv, y_sem, y_send, y_recv,
):
    rows = y.shape[0]
    half = rows // 2
    piece = half // 2
    tiles = y.shape[1] // COLS
    phases = 2 * tiles
    chunks = x.shape[1] // DEPTH
    ctx_depth = ctx.shape[1]
    ctx_chunks = ctx_depth // DEPTH

    me = lax.axis_index("tp")
    core = lax.rem(me, 2)
    sib = {"tp": me + 1 - 2 * core}
    far = {"tp": lax.rem(me + 2, 4)}
    own_row = pl.multiple_of(core * half, half)
    sib_row = pl.multiple_of((1 - core) * half, half)

    def columns(p):
        return pl.ds(pl.multiple_of(lax.rem(p, tiles) * COLS, COLS), COLS)

    def load_x(h, side, i):
        row = pl.multiple_of((sib_row if side == 0 else own_row) + h * piece, piece)
        if i < ctx_chunks:
            src = ctx.at[pl.ds(row, piece), pl.ds(i * DEPTH, DEPTH)]
        else:
            src = act.at[pl.ds(row, piece), pl.ds((i - ctx_chunks) * DEPTH, DEPTH)]
        dst = x.at[pl.ds(side * piece, piece), pl.ds(i * DEPTH, DEPTH)]
        return pltpu.make_async_copy(src, dst, x_sem.at[side, i])

    def load_w(p):
        s = lax.rem(p, 2)
        return (
            pltpu.make_async_copy(
                w_out.at[:, columns(p)], w.at[s, pl.ds(0, ctx_depth), :], w_sem.at[s, 0]),
            pltpu.make_async_copy(
                w_down.at[:, columns(p)], w.at[s, pl.ds(ctx_depth, w_down.shape[0]), :],
                w_sem.at[s, 1]),
        )

    def send_part(p):
        return pltpu.make_async_remote_copy(
            part.at[lax.rem(p, 2)], sib_part.at[lax.rem(p, 4)],
            sib_send.at[lax.rem(p, 2)], sib_recv.at[lax.rem(p, 4)],
            device_id=sib, device_id_type=MESH)

    def send_chip(p):
        s = lax.rem(p, SLOTS)
        return pltpu.make_async_remote_copy(
            chip.at[s], far_chip.at[s], far_send.at[s], far_recv.at[s],
            device_id=far, device_id_type=MESH)

    def y_block(p):
        row = pl.multiple_of(own_row + p // tiles * piece, piece)
        return y.at[pl.ds(row, piece), columns(p)]

    def store_y(p):
        s = lax.rem(p, 2)
        return pltpu.make_async_copy(done.at[s], y_block(p), y_sem.at[s])

    def send_y(p):
        s = lax.rem(p, 2)
        return pltpu.make_async_remote_copy(
            done.at[s], y_block(p), y_send.at[s], y_recv.at[lax.rem(p, 4)],
            device_id=sib, device_id_type=MESH)

    def chip_sum(p):
        total = acc[lax.rem(p, 2)] + sib_part[lax.rem(p, 4)].astype(jnp.float32)
        chip[lax.rem(p, SLOTS)] = total.astype(jnp.bfloat16)

    def final_sum(p):
        s = lax.rem(p, SLOTS)
        total = chip[s].astype(jnp.float32) + far_chip[s].astype(jnp.float32)
        done[lax.rem(p, 2)] = total.astype(jnp.bfloat16)

    def finish_chip(p):
        send_part(p).wait_recv()

        @pl.when(p >= SLOTS)
        def _():
            send_chip(p - SLOTS).wait_send()

        chip_sum(p)
        send_chip(p).start()

    def wait_final(p):
        send_chip(p).wait_recv()

        @pl.when(p >= 2)
        def _():
            store_y(p - 2).wait()
            send_y(p - 2).wait_send()
            send_y(p - 2).wait_recv()

    def start_y(p):
        store_y(p).start()
        send_y(p).start()

    def dot(side, depth, slot):
        return jnp.dot(x[pl.ds(side * piece, piece), depth], w[slot, depth, :],
                       preferred_element_type=jnp.float32)

    first_w = load_w(0)
    first_w[0].start()
    for i in range(chunks):
        for side in range(2):
            load_x(0, side, i).start()
        if i == 0:
            first_w[1].start()

    barrier = pltpu.get_barrier_semaphore()
    for peer in (sib, far):
        pl.semaphore_signal(barrier, inc=1, device_id=peer, device_id_type=MESH)
    pl.semaphore_wait(barrier, 2)

    def prepare(p, with_final):
        @pl.when(p >= 2)
        def _():
            finish_chip(p - 2)
            send_part(p - 2).wait_send()

        if with_final:
            wait_final(p - LAG)

        @pl.when(p + 1 < phases)
        def _():
            for copy in load_w(p + 1):
                copy.start()

    def whole(p, with_final):
        for copy in load_w(p):
            copy.wait()
        prepare(p, with_final)
        s = lax.rem(p, 2)
        if with_final:
            final_sum(p - LAG)
        everything = pl.ds(0, x.shape[1])
        part[s] = dot(0, everything, s).astype(jnp.bfloat16)
        acc[s] = dot(1, everything, s)
        send_part(p).start()
        if with_final:
            start_y(p - LAG)

    def chunked(p, arrives, leaves, with_final):
        copies = load_w(p)
        copies[0].wait()
        if p > 0:
            copies[1].wait()
        prepare(p, with_final)
        s = p % 2
        for i in range(chunks):
            if arrives:
                for side in range(2):
                    load_x(p // tiles, side, i).wait()
            if p == 0 and i == 1:
                copies[1].wait()
            depth = pl.ds(i * DEPTH, DEPTH)
            sib_term, own_term = dot(0, depth, s), dot(1, depth, s)
            if i == 0:
                sib_acc[...] = sib_term
                acc[s] = own_term
            else:
                sib_acc[...] += sib_term
                acc[s] += own_term
            if leaves:
                for side in range(2):
                    load_x(p // tiles + 1, side, i).start()
        part[s] = sib_acc[...].astype(jnp.bfloat16)
        send_part(p).start()
        if with_final:
            final_sum(p - LAG)
            start_y(p - LAG)

    def early(p, carry):
        whole(p, False)
        return carry

    def steady(p, carry):
        whole(p, True)
        return carry

    chunked(0, True, False, False)
    lax.fori_loop(1, LAG, early, 0)
    lax.fori_loop(LAG, tiles - 1, steady, 0)
    chunked(tiles - 1, False, True, True)
    chunked(tiles, True, False, True)
    lax.fori_loop(tiles + 1, phases, steady, 0)

    for p in range(phases - 2, phases):
        finish_chip(p)
    for p in range(phases - LAG, phases):
        wait_final(p)
        final_sum(p)
        start_y(p)
    for p in range(phases - 2, phases):
        store_y(p).wait()
        send_y(p).wait_send()
        send_y(p).wait_recv()
        send_part(p).wait_send()
    for p in range(phases - SLOTS, phases):
        send_chip(p).wait_send()


def solution(mesh):
    def device_step(ctx, w_out, act, w_down):
        rows, depth = ctx.shape[0], ctx.shape[1] + act.shape[1]
        width = w_out.shape[1]
        piece = (rows // 4, COLS)
        sem = pltpu.SemaphoreType.DMA
        bf16, f32 = jnp.bfloat16, jnp.float32
        return pl.pallas_call(
            _kernel,
            out_shape=jax.ShapeDtypeStruct((rows, width), bf16),
            in_specs=[pl.BlockSpec(memory_space=pl.ANY)] * 4,
            out_specs=pl.BlockSpec(memory_space=pl.ANY),
            scratch_shapes=[
                pltpu.VMEM((rows // 2, depth), bf16),
                pltpu.VMEM((2, depth, COLS), bf16),
                pltpu.VMEM(piece, f32),
                pltpu.VMEM((2, *piece), f32),
                pltpu.VMEM((2, *piece), bf16),
                pltpu.VMEM((4, *piece), bf16),
                pltpu.VMEM((SLOTS, *piece), bf16),
                pltpu.VMEM((SLOTS, *piece), bf16),
                pltpu.VMEM((2, *piece), bf16),
                sem((2, depth // DEPTH)), sem((2, 2)),
                sem((2,)), sem((4,)),
                sem((SLOTS,)), sem((SLOTS,)),
                sem((2,)), sem((2,)), sem((4,)),
            ],
            compiler_params=pltpu.CompilerParams(
                collective_id=0, has_side_effects=True, vmem_limit_bytes=67043328),
            cost_estimate=pl.CostEstimate(
                flops=2 * rows * depth * width, transcendentals=0,
                bytes_accessed=2 * (rows * depth + depth * width + rows * width)),
        )(ctx, w_out, act, w_down)

    return jax.shard_map(
        device_step,
        mesh=mesh,
        in_specs=(P("data", "tp"), P("tp", None), P("data", "tp"), P("tp", None)),
        out_specs=P("data", None),
        check_vma=False,
    )
```

time: 852 us -> 414 us (0.49)
  waiting for transfers between devices: 430 us -> 0 us
  Pallas kernels: 0 us -> 390 us
  matrix products: 385 us -> 0 us
  between operations: 13.4 us -> 0.01 us
    pallas_call x0 -> x1, Pallas kernels: none -> 390 us  [device_step(): pl.pallas_call(_kernel, out_shape=jax.ShapeDtypeStruct((rows, width), bf1...]
    dot_general x2 -> x0, matrix products: 385 us -> none  [the longest x1 306 us: device_step(): jnp.dot(act_block, w_down_block, preferred_element_type=jnp.float32)]
    unnamed x3 -> x0, waiting for transfers between devices: 229 us -> none
    all_gather x1 -> x0, waiting for transfers between devices: 201 us -> none  [device_step(): return lax.all_gather(row_sum, 'tp', axis=0, tiled=True)]
  transfers between devices with their start and end apart: 2 -> 0, of which waited for: 2 -> 0; matrix products, arithmetic and copies ran while one was open for 0% -> 0% of each run, Pallas kernels for 0% -> 0%
where the time goes in v2:
time: 414 us; the launch traced here: 413 us
  Pallas kernels  390 us (94%)
  local copies, waits for them, and re-layouts  23 us (6%)
    pallas_call x1, Pallas kernels, device_step(): pl.pallas_call(_kernel, out_shape=jax.ShapeDtypeStruct((rows, width), bf1...  390 us
    unnamed x1, local copies, waits for them, and re-layouts  23 us

profile of v2, /device:TPU:0, one launch (start us, length us, event | category | flops | bytes accessed | tf_op | source)
XLA Modules:
  0.0 413.5 jit_solution(2614557366998468671)
XLA Ops:
  0.0 390.5 %shard_map.46 = bf16[2048,8192]{1,0:T(8,128)(2,1)} custom-call(bf16[2048,2048]{1,0:T(8,128)(2,1)} %ctx.1, bf16[2048,8192]{1,0:T(8,128)(2,1)} %w_out.1, bf16[2048,8192]{1,0:T(8,128)(2,1)} %act.1, bf16[8192,8192]{1,0:T(8,128)(2,1)} %w_down.1), custom_call_target="tpu_custom_call" | custom-call | flops 343597383680 | bytes 243269632 | tf_op jit(solution)/shard_map/pallas_call | solution.py:228
  390.5 23.0 %copy.6 = bf16[2048,8192]{1,0:T(8,128)(2,1)} copy(bf16[2048,8192]{1,0:T(8,128)(2,1)} %shard_map.46) | data formatting | bytes 67108864
